TPU v7x, 32 devices: a whole 2x2x4 slice. The times are simulated.
32 devices in a mesh: expert: 16 (over z, y, core), tensor: 2 (over x).
Axes of the slice: x: 2, y: 2, z: 4, core: 2. Of those that a mesh axis runs over, the one named last changes fastest.
Arguments:
- tokens: bfloat16 [64, 256, 1280], P(('expert', 'tensor')), may hold values from -6 to 6
- slot_keys: bfloat16 [1280, 16], replicated, may hold values from -6 to 6
- logit_scale: float32 [], replicated, may hold values from 40 to 80
- w_in: bfloat16 [16, 1280, 3584], P('expert', None, 'tensor'), may hold values from -0.625 to 0.625
- b_in: bfloat16 [16, 3584], P('expert', 'tensor'), may hold values from -3 to 3
- w_out: bfloat16 [16, 3584, 1280], P('expert', 'tensor'), may hold values from -0.09375 to 0.09375
- b_out: bfloat16 [16, 1280], P('expert'), may hold values from -3 to 3
Outputs:
- mixed: bfloat16 [64, 256, 1280], P(('expert', 'tensor'))
All inputs are finite; a program needn't handle non-finite values.
Results may differ from a plain program's by a relative error of at most 0.0071.
Values may be sent and summed in bfloat16 or wider, within the bound.
A program may use at most 64 MiB of HBM per device.

v0:
```python
import jax
import jax.numpy as jnp
from jax import lax
from jax.sharding import PartitionSpec as P

EPS = 1e-06


def local(tokens, slot_keys, logit_scale, w_in, b_in, w_out, b_out):
    images, seq_len, width = tokens.shape
    slots = slot_keys.shape[1]
    row_sq = jnp.sum(jnp.square(tokens.astype(jnp.float32)), axis=2, keepdims=True)
    row_inv = lax.rsqrt(row_sq + EPS)
    key_sq = jnp.sum(jnp.square(slot_keys.astype(jnp.float32)), axis=0)
    key_inv = lax.rsqrt(key_sq + EPS)
    raw = jnp.dot(
        tokens.reshape(images * seq_len, width), slot_keys, preferred_element_type=jnp.float32
    )
    logits = logit_scale * row_inv * key_inv * raw.reshape(images, seq_len, slots)
    expo = jnp.exp(logits)
    dispatch = (expo / jnp.sum(expo, axis=1, keepdims=True)).astype(jnp.bfloat16)
    combine = (expo / jnp.sum(expo, axis=2, keepdims=True)).astype(jnp.bfloat16)
    slot_in = jnp.einsum(
        "ims,imd->isd", dispatch, tokens, preferred_element_type=jnp.float32
    ).astype(jnp.bfloat16)
    routed = lax.all_to_all(slot_in, "expert", split_axis=1, concat_axis=0, tiled=True)
    bias_wide = b_in.astype(jnp.float32)
    pre = (
        jnp.einsum(
            "rkd,kdf->rkf",
            lax.all_gather(routed, "tensor", axis=0, tiled=True),
            w_in,
            preferred_element_type=jnp.float32,
        )
        + bias_wide[None]
    )
    hidden = jax.nn.gelu(pre).astype(jnp.bfloat16)
    mine = lax.psum_scatter(
        jnp.einsum("rkf,kfd->rkd", hidden, w_out, preferred_element_type=jnp.float32),
        "tensor",
        scatter_dimension=0,
        tiled=True,
    )
    slot_out = (mine + b_out.astype(jnp.float32)[None]).astype(jnp.bfloat16)
    returned = lax.all_to_all(slot_out, "expert", split_axis=0, concat_axis=1, tiled=True)
    mixed = jnp.einsum("ims,isd->imd", combine, returned, preferred_element_type=jnp.float32)
    return mixed.astype(jnp.bfloat16)


def solution(mesh):
    placed = (
        P(("expert", "tensor"), None, None),
        P(),
        P(),
        P("expert", None, "tensor"),
        P("expert", "tensor"),
        P("expert", "tensor", None),
        P("expert", None),
    )
    return jax.shard_map(
        local,
        mesh=mesh,
        in_specs=placed,
        out_specs=P(("expert", "tensor"), None, None),
        check_vma=False,
    )
```

profile of v0, /device:TPU:0, one launch (start us, length us, event | category | flops | bytes accessed | tf_op | source)
XLA Modules:
  0.0 72.5 jit_solution(5864950734486424679)
XLA Ops:
  6.5 0.0 copy-start
  6.5 0.0 copy-start.1
  7.3 0.9 %multiply_reduce_fusion.1 = f32[16]{0:T(128)S(1)} fusion(bf16[1280,16]{0,1:T(8,128)(2,1)} %param.8), kind=kLoop, calls=%fused_computation.32 | loop fusion | flops 61424 | bytes 41024 | tf_op jit(solution)/shard_map/reduce_sum | solution.py:14
  8.2 1.7 %multiply_reduce_fusion = f32[2,256]{1,0:T(2,128)S(1)} fusion(bf16[2,256,1280]{2,1,0:T(8,128)(2,1)} %param.7), kind=kLoop, calls=%fused_computation.5 | loop fusion | flops 1965568 | bytes 1312768 | tf_op jit(solution)/shard_map/reduce_sum | solution.py:12
  9.9 1.8 %fusion.16 = f32[2,256,16]{1,2,0:T(8,128)S(1)} fusion(bf16[2,256,1280]{2,1,0:T(8,128)(2,1)} %param.7, bf16[1280,16]{0,1:T(8,128)(2,1)} %param.8, f32[16]{0:T(128)S(1)} %add_rsqrt_fusion, f32[2,256]{1,0:T(2,128)S(1)} %rsqrt_multiply_fusion), kind=kOutput, calls=%fused_computation.12 | convolution fusion | flops 20987904 | bytes 1386560 | tf_op jit(solution)/shard_map/dot_general | solution.py:16
  11.7 0.0 copy-done
  11.7 0.3 convolution_convert_fusion.1
  12.0 0.7 copy.13
  12.7 7.4 %all-to-all-start = ((bf16[2,16,1280]{2,0,1:T(2,128)(2,1)}), bf16[2,16,1280]{2,0,1:T(2,128)(2,1)S(1)}, u32[]{:S(2)}, u32[]{:S(2)}) async-start(bf16[2,16,1280]{2,0,1:T(2,128)(2,1)} %copy.13), calls=%async_computation | async-start | bytes 163840 | tf_op jit(solution)/shard_map/all_to_all | solution.py:26
  20.1 0.0 reduce-scatter.2.cloned.1.call-start
  20.2 0.0 copy-done.1
  20.2 7.0 %all-to-all-done = bf16[2,16,1280]{2,0,1:T(2,128)(2,1)S(1)} async-done(((bf16[2,16,1280]{2,0,1:T(2,128)(2,1)}), bf16[2,16,1280]{2,0,1:T(2,128)(2,1)S(1)}, u32[]{:S(2)}, u32[]{:S(2)}) %all-to-all-start) | async-done | bytes 81952 | tf_op jit(solution)/shard_map/all_to_all | solution.py:26
  27.3 5.1 %all_gather.3 = bf16[64,1,1280]{2,0,1:T(8,128)(2,1)S(1)} all-gather(bf16[32,1,1280]{2,0,1:T(8,128)(2,1)S(1)} %all_to_all.29), channel_id=1, replica_groups=mesh['expert'=16,'tensor'=2] {'tensor'}, dimensions={0}, use_global_device_ids=true | all-gather | bytes 245760 | tf_op jit(solution)/shard_map/all_gather | solution.py:31
  32.4 0.0 copy-start.2
  32.4 6.3 %fusion.4 = f32[64,1,1280]{2,0,1:T(8,128)} fusion(bf16[1,1792,1280]{2,1,0:T(8,128)(2,1)} %param.12, bf16[1,1280,1792]{2,1,0:T(8,128)(2,1)} %param.10, f32[1792]{0:T(1024)S(1)} %convert_reduce_fusion, bf16[64,1,1280]{2,0,1:T(8,128)(2,1)S(1)} %all_gather.3), kind=kOutput, calls=%fused_computation.6 | convolution fusion | flops 588349440 | bytes 9673728 | tf_op jit(solution)/shard_map/rkf,kfd->rkd/dot_general | solution.py:39
  38.7 0.0 reduce-scatter.2.cloned.1.call-update
  38.7 0.0 copy-done.2
  38.7 10.0 %reduce-scatter.2.cloned.1.call-done = f32[32,1,1280]{2,0,1:T(8,128)} async-done(((f32[64,1,1280]{2,0,1:T(8,128)}), f32[32,1,1280]{2,0,1:T(8,128)}) %reduce-scatter.2.cloned.1.call-update) | async-done | bytes 163856 | tf_op jit(solution)/shard_map/reduce_scatter | solution.py:38
  48.7 0.9 %add_convert_fusion = bf16[32,1,1280]{2,0,1:T(8,128)(2,1)S(1)} fusion(f32[32,1,1280]{2,0,1:T(8,128)} %reduce-scatter.2.cloned.1.call-done, f32[1280]{0:T(1024)S(1)} %convert_reduce_fusion.1), kind=kLoop, calls=%fused_computation.29 | loop fusion | flops 81920 | bytes 250880 | tf_op jit(solution)/shard_map/convert_element_type | solution.py:44
  49.7 0.5 broadcast.27
  50.2 0.7 reduce.5
  50.9 12.5 %all_to_all.36 = bf16[16,2,1280]{2,1,0:T(2,128)(2,1)S(1)} all-to-all(bf16[16,2,1280]{2,1,0:T(2,128)(2,1)S(1)} %reshape.50), channel_id=1, replica_groups=mesh['expert'=16,'tensor'=2] {'expert'}, dimensions={0} | all-to-all | bytes 163840 | tf_op jit(solution)/shard_map/all_to_all | solution.py:45
  63.4 0.1 reshape.51
  63.5 0.5 reduce.2
  64.0 1.6 %convolution_convert_fusion = bf16[2,256,1280]{2,1,0:T(8,128)(2,1)} fusion(bf16[16,2,1,1280]{3,1,0,2:T(2,128)(2,1)S(1)} %all_to_all.31, f32[2,256,16]{1,2,0:T(8,128)S(1)} %fusion.16), kind=kOutput, calls=%fused_computation.4 | convolution fusion | flops 21643792 | bytes 1425408 | tf_op jit(solution)/shard_map/ims,isd->imd/dot_general | solution.py:46
  (7 shorter events, 0.2 us)
Async XLA Ops:
  6.5 5.1 %copy-start = (bf16[2,256,1280]{2,1,0:T(8,128)(2,1)S(1)}, bf16[2,256,1280]{2,1,0:T(8,128)(2,1)}, u32[]{:S(2)}) copy-start(bf16[2,256,1280]{2,1,0:T(8,128)(2,1)} %param.7) | copy-start | bytes 3932164
  6.5 13.6 %copy-start.1 = (bf16[1,1792]{1,0:T(2,128)(2,1)S(1)}, bf16[1,1792]{1,0:T(2,128)(2,1)}, u32[]{:S(2)}) copy-start(bf16[1,1792]{1,0:T(2,128)(2,1)} %param.11) | copy-start | bytes 10756
  12.7 14.5 %all-to-all-start = ((bf16[2,16,1280]{2,0,1:T(2,128)(2,1)}), bf16[2,16,1280]{2,0,1:T(2,128)(2,1)S(1)}, u32[]{:S(2)}, u32[]{:S(2)}) async-start(bf16[2,16,1280]{2,0,1:T(2,128)(2,1)} %copy.13), calls=%async_computation | async-start | bytes 163840 | tf_op jit(solution)/shard_map/all_to_all | solution.py:26
  20.1 28.6 %reduce-scatter.2.cloned.1.call-start = ((), (), s32[]{:S(2)}) async-start(), calls=%async_computation.3 | async-start | bytes 491520 | tf_op jit(solution)/shard_map/reduce_scatter | solution.py:38
  32.4 6.3 %copy-start.2 = (bf16[1,1280]{1,0:T(2,128)(2,1)S(1)}, bf16[1,1280]{1,0:T(2,128)(2,1)}, u32[]{:S(2)}) copy-start(bf16[1,1280]{1,0:T(2,128)(2,1)} %param.13) | copy-start | bytes 7684
Sparse Core Ops, SparseCore 0:
  38.8 9.8 reduce-scatter.1
where the time goes:
time: 72.8 us; the launch traced here: 72.5 us
  blocking collectives  17.6 us (24%)
  waiting for transfers between devices  17.1 us (23%)
  between operations  14.3 us (20%)
  matrix products  9.99 us (14%)
  starting transfers between devices  7.46 us (10%)
  other arithmetic  4.67 us (6%)
  local copies, waits for them, and re-layouts  1.4 us (2%)
    all_to_all x1, blocking collectives, local(): lax.all_to_all(slot_out, 'expert', split_axis=0, concat_axis=1, tiled=True)  12.5 us
    reduce_scatter x1, waiting for transfers between devices, local(): lax.psum_scatter(jnp.einsum('rkf,kfd->rkd', hidden, w_out, preferred_elem...  10 us
    all_to_all x1, starting transfers between devices, local(): lax.all_to_all(slot_in, 'expert', split_axis=1, concat_axis=0, tiled=True)  7.41 us
    all_to_all x1, waiting for transfers between devices, local(): lax.all_to_all(slot_in, 'expert', split_axis=1, concat_axis=0, tiled=True)  7.02 us
    dot_general x1, matrix products, local(): jnp.einsum('rkf,kfd->rkd', hidden, w_out, preferred_element_type=jnp.floa...  6.26 us
    all_gather x1, blocking collectives, local(): lax.all_gather(routed, 'tensor', axis=0, tiled=True)  5.11 us
    dot_general x1, matrix products, local(): jnp.dot(tokens.reshape(images * seq_len, width), slot_keys, preferred_ele...  1.78 us
    reduce_sum x1, other arithmetic, local(): jnp.sum(jnp.square(tokens.astype(jnp.float32)), axis=2, keepdims=True)  1.65 us
  transfers between devices with their start and end apart: 2, of which 2 were waited for; matrix products, arithmetic and copies ran while one was open for 0% of the time, Pallas kernels for 0%

commit v1 on v0

v1 whole, which is shorter than its diff:
```python
import functools

import jax
import jax.numpy as jnp
from jax import lax
from jax.experimental import pallas as pl
from jax.experimental.pallas import tpu as pltpu
from jax.sharding import PartitionSpec as P

EPS = 1e-06
MESH = pl.DeviceIdType.MESH
NT = (((1,), (1,)), ((), ()))


def column_cuts(width):
    first = (width * 3 // 5) // 256 * 256
    return [(0, first), (first, width - first)] if 0 < first < width else [(0, width)]


def kernel(
    experts, tensors, cuts,
    tokens_hbm, keys_ref, scale_ref, w_in_hbm, b_in_ref, w_out_hbm, b_out_ref,
    out_ref,
    tok, w_in, w_out, send1, recv1, x2, hidden, comb, *rest,
):
    n_cut = len(cuts)
    send2, recv2 = rest[:n_cut], rest[n_cut:2 * n_cut]
    load_sem, send_sem1, recv_sem1, send_sem2, recv_sem2 = rest[2 * n_cut:]
    images, seq, width = tok.shape
    slots = keys_ref.shape[1]
    rows = slots * images
    devices = experts * tensors
    e, t = lax.axis_index("expert"), lax.axis_index("tensor")
    me = e * tensors + t
    home = t * experts + e

    loads = [
        pltpu.make_async_copy(tokens_hbm, tok, load_sem.at[0]),
        pltpu.make_async_copy(w_in_hbm.at[0], w_in, load_sem.at[1]),
        pltpu.make_async_copy(w_out_hbm.at[0], w_out, load_sem.at[2]),
    ]
    for load in loads:
        load.start()

    def peer(step):
        j = lax.rem(me + step, devices)
        je, jt = j // tensors, lax.rem(j, tensors)
        return j, je, {"expert": je, "tensor": jt}

    barrier = pltpu.get_barrier_semaphore()

    @pl.loop(1, devices)
    def _(step):
        pl.semaphore_signal(barrier, inc=1, device_id=peer(step)[2], device_id_type=MESH)

    row_slot = lax.broadcasted_iota(jnp.int32, (rows, slots), 0) // images
    col_slot = lax.broadcasted_iota(jnp.int32, (rows, slots), 1)
    spread = jnp.where(row_slot == col_slot, 1.0, 0.0).astype(jnp.bfloat16)
    keys_t = lax.dot_general(spread, keys_ref[...], NT, preferred_element_type=jnp.float32)
    key_inv = lax.rsqrt(jnp.sum(keys_t * keys_t, axis=1, keepdims=True) + EPS)
    key_gain = key_inv * scale_ref[0]
    keys_b = keys_t.astype(jnp.bfloat16)

    loads[0].wait()
    flat = tok[...].reshape(images * seq, width)
    raw = lax.dot_general(keys_b, flat, NT, preferred_element_type=jnp.float32)
    part = jnp.zeros((images * seq, 128), jnp.float32)
    for c in range(width // 128):
        piece = flat[:, c * 128:(c + 1) * 128].astype(jnp.float32)
        part = part + piece * piece
    row_sq = lax.dot_general(
        jnp.ones((8, 128), jnp.float32), part, NT,
        precision=lax.Precision.HIGHEST, preferred_element_type=jnp.float32,
    )[0:1]
    logits = key_gain * lax.rsqrt(row_sq + EPS) * raw
    row_image = lax.broadcasted_iota(jnp.int32, logits.shape, 0) % images
    col_image = lax.broadcasted_iota(jnp.int32, logits.shape, 1) // seq
    expo = jnp.where(row_image == col_image, jnp.exp(logits), 0.0)
    dispatch = (expo / jnp.sum(expo, axis=1, keepdims=True)).astype(jnp.bfloat16)
    slot_in = jnp.dot(dispatch, flat, preferred_element_type=jnp.float32).astype(jnp.bfloat16)
    for s in range(slots):
        send1[s] = slot_in[s * images:(s + 1) * images]

    pl.semaphore_wait(barrier, devices - 1)

    own = pltpu.make_async_copy(send1.at[e], recv1.at[me], recv_sem1)
    own.start()

    @pl.loop(1, devices)
    def _(step):
        _, je, device = peer(step)
        pltpu.make_async_remote_copy(
            src_ref=send1.at[je], dst_ref=recv1.at[me], send_sem=send_sem1, recv_sem=recv_sem1,
            device_id=device, device_id_type=MESH,
        ).start()

    combine = expo / jnp.sum(expo, axis=0, keepdims=True)
    comb[...] = jnp.concatenate([combine] * tensors, axis=0).T.astype(jnp.bfloat16)

    loads[1].wait()
    pltpu.make_async_copy(recv1, recv1, recv_sem1).wait()
    for k in range(devices):
        x2[k * images:(k + 1) * images, :] = recv1[k]
    x = x2[...]
    half = w_in.shape[1]
    for c in range(0, half, 256):
        size = min(256, half - c)
        pre = jnp.dot(x, w_in[:, c:c + size], preferred_element_type=jnp.float32)
        pre = pre + b_in_ref[:, c:c + size].astype(jnp.float32)
        hidden[:, c:c + size] = jax.nn.gelu(pre).astype(jnp.bfloat16)

    loads[2].wait()
    h = hidden[...]
    first_half = jnp.where(t == 0, 1.0, 0.0)
    for c, (start, size) in enumerate(cuts):
        y = jnp.dot(h, w_out[:, start:start + size], preferred_element_type=jnp.float32)
        y = y + b_out_ref[:, start:start + size].astype(jnp.float32) * first_half
        y = y.astype(jnp.bfloat16)
        for k in range(devices):
            send2[c][k] = y[k * images:(k + 1) * images]
        pltpu.make_async_copy(send2[c].at[me], recv2[c].at[home], recv_sem2.at[c]).start()

        @pl.loop(1, devices)
        def _(step):
            j, _, device = peer(step)
            pltpu.make_async_remote_copy(
                src_ref=send2[c].at[j], dst_ref=recv2[c].at[home],
                send_sem=send_sem2.at[c], recv_sem=recv_sem2.at[c],
                device_id=device, device_id_type=MESH,
            ).start()

    cm = comb[...]
    for c, (start, size) in enumerate(cuts):
        pltpu.make_async_copy(recv2[c], recv2[c], recv_sem2.at[c]).wait()
        for k in range(devices):
            x2[k * images:(k + 1) * images, start:start + size] = recv2[c][k]
        mixed = jnp.dot(cm, x2[:, start:start + size], preferred_element_type=jnp.float32)
        out_ref[:, :, start:start + size] = mixed.astype(jnp.bfloat16).reshape(images, seq, size)

    first = recv1.at[pl.ds(0, devices - 1)]
    pltpu.make_async_copy(first, first, send_sem1).wait()
    for c in range(n_cut):
        block = recv2[c].at[pl.ds(0, devices - 1)]
        pltpu.make_async_copy(block, block, send_sem2.at[c]).wait()


def local(experts, tensors, tokens, slot_keys, logit_scale, w_in, b_in, w_out, b_out):
    images, seq, width = tokens.shape
    slots = slot_keys.shape[1]
    half = w_in.shape[2]
    devices = experts * tensors
    cuts = column_cuts(width)
    bf16 = jnp.bfloat16
    return pl.pallas_call(
        functools.partial(kernel, experts, tensors, cuts),
        out_shape=jax.ShapeDtypeStruct(tokens.shape, bf16),
        in_specs=[
            pl.BlockSpec(memory_space=pl.ANY),
            pl.BlockSpec(memory_space=pltpu.VMEM),
            pl.BlockSpec(memory_space=pltpu.SMEM),
            pl.BlockSpec(memory_space=pl.ANY),
            pl.BlockSpec(memory_space=pltpu.VMEM),
            pl.BlockSpec(memory_space=pl.ANY),
            pl.BlockSpec(memory_space=pltpu.VMEM),
        ],
        out_specs=pl.BlockSpec(memory_space=pltpu.VMEM),
        scratch_shapes=[
            pltpu.VMEM((images, seq, width), bf16),
            pltpu.VMEM((width, half), bf16),
            pltpu.VMEM((half, width), bf16),
            pltpu.VMEM((slots, images, width), bf16),
            pltpu.VMEM((devices, images, width), bf16),
            pltpu.VMEM((devices * images, width), bf16),
            pltpu.VMEM((devices * images, half), bf16),
            pltpu.VMEM((images * seq, tensors * slots * images), bf16),
            *[pltpu.VMEM((devices, images, size), bf16) for _, size in cuts],
            *[pltpu.VMEM((devices, images, size), bf16) for _, size in cuts],
            pltpu.SemaphoreType.DMA((3,)),
            pltpu.SemaphoreType.DMA,
            pltpu.SemaphoreType.DMA,
            pltpu.SemaphoreType.DMA((len(cuts),)),
            pltpu.SemaphoreType.DMA((len(cuts),)),
        ],
        compiler_params=pltpu.CompilerParams(collective_id=0, has_side_effects=True),
    )(tokens, slot_keys, logit_scale.reshape(1), w_in, b_in, w_out, b_out)


def solution(mesh):
    placed = (
        P(("expert", "tensor"), None, None),
        P(),
        P(),
        P("expert", None, "tensor"),
        P("expert", "tensor"),
        P("expert", "tensor", None),
        P("expert", None),
    )
    return jax.shard_map(
        functools.partial(local, mesh.shape["expert"], mesh.shape["tensor"]),
        mesh=mesh,
        in_specs=placed,
        out_specs=P(("expert", "tensor"), None, None),
        check_vma=False,
    )
```

time: 72.8 us -> 28.3 us (0.39)
  Pallas kernels: 0 us -> 23.3 us
  blocking collectives: 17.6 us -> 0 us
  waiting for transfers between devices: 17.1 us -> 0 us
  between operations: 14.3 us -> 0.66 us
  matrix products: 9.99 us -> 0 us
  starting transfers between devices: 7.46 us -> 0 us
  other arithmetic: 4.67 us -> 0 us
  local copies, waits for them, and re-layouts: 1.4 us -> 4.13 us
    pallas_call x0 -> x1, Pallas kernels: none -> 23.3 us  [local(): pl.pallas_call(functools.partial(kernel, experts, tensors, cuts), out_sha...]
    all_to_all x1 -> x0, blocking collectives: 12.5 us -> none  [local(): lax.all_to_all(slot_out, 'expert', split_axis=0, concat_axis=1, tiled=True)]
    reduce_scatter x1 -> x0, waiting for transfers between devices: 10 us -> none  [local(): lax.psum_scatter(jnp.einsum('rkf,kfd->rkd', hidden, w_out, preferred_elem...]
    dot_general x4 -> x0, matrix products: 9.99 us -> none  [the longest x1 6.26 us: local(): jnp.einsum('rkf,kfd->rkd', hidden, w_out, preferred_element_type=jnp.floa...]
    all_to_all x1 -> x0, starting transfers between devices: 7.41 us -> none  [local(): lax.all_to_all(slot_in, 'expert', split_axis=1, concat_axis=0, tiled=True)]
    all_to_all x1 -> x0, waiting for transfers between devices: 7.02 us -> none  [local(): lax.all_to_all(slot_in, 'expert', split_axis=1, concat_axis=0, tiled=True)]
    all_gather x1 -> x0, blocking collectives: 5.11 us -> none  [local(): lax.all_gather(routed, 'tensor', axis=0, tiled=True)]
    unnamed x8 -> x2, local copies, waits for them, and re-layouts: 0.11 us -> 4.13 us
  transfers between devices with their start and end apart: 2 -> 0, of which waited for: 2 -> 0; matrix products, arithmetic and copies ran while one was open for 0% -> 0% of each run, Pallas kernels for 0% -> 0%
where the time goes in v1:
time: 28.3 us; the launch traced here: 28.1 us
  Pallas kernels  23.3 us (82%)
  local copies, waits for them, and re-layouts  4.13 us (15%)
  between operations  0.66 us (2%)
    pallas_call x1, Pallas kernels, local(): pl.pallas_call(functools.partial(kernel, experts, tensors, cuts), out_sha...  23.3 us
    unnamed x2, local copies, waits for them, and re-layouts  4.13 us

profile of v1, /device:TPU:0, one launch (start us, length us, event | category | flops | bytes accessed | tf_op | source)
XLA Modules:
  0.0 28.1 jit_solution(1754020460258786325)
XLA Ops:
  0.7 1.7 %copy.8.keys_ref = bf16[1280,16]{1,0:T(8,128)(2,1)} copy(bf16[1280,16]{0,1:T(8,128)(2,1)} %param.8) | data formatting | bytes 81920 | tf_op args[1]
  2.3 23.3 %shard_map.73 = bf16[2,256,1280]{2,1,0:T(8,128)(2,1)} custom-call(bf16[2,256,1280]{2,1,0:T(8,128)(2,1)} %tokens_hbm.1, bf16[1280,16]{1,0:T(8,128)(2,1)} %copy.8.keys_ref, f32[1]{0:T(128)} %bitcast.1.scale_ref, bf16[1,1280,1792]{2,1,0:T(8,128)(2,1)} %w_in_hbm.1, bf16[1,1792]{1,0:T(2,128)(2,1)} %b_in_ref.1, bf16[1,1792,1280]{2,1,0:T(8,128)(2,1)} %w_out_hbm.1, ...), custom_call_target="tpu_custom_call" | custom-call | tf_op jit(solution)/shard_map/pallas_call | solution.py:154
  25.7 2.5 %copy.11 = bf16[2,256,1280]{2,1,0:T(8,128)(2,1)} copy(bf16[2,256,1280]{2,1,0:T(8,128)(2,1)} %shard_map.73) | data formatting | bytes 2621440

commit v2 on v1

--- a/solution.py
+++ b/solution.py
@@ -27,7 +27,7 @@
     send2, recv2 = rest[:n_cut], rest[n_cut:2 * n_cut]
     load_sem, send_sem1, recv_sem1, send_sem2, recv_sem2 = rest[2 * n_cut:]
     images, seq, width = tok.shape
-    slots = keys_ref.shape[1]
+    slots = keys_ref.shape[0]
     rows = slots * images
     devices = experts * tensors
     e, t = lax.axis_index("expert"), lax.axis_index("tensor")
@@ -56,7 +56,7 @@
     row_slot = lax.broadcasted_iota(jnp.int32, (rows, slots), 0) // images
     col_slot = lax.broadcasted_iota(jnp.int32, (rows, slots), 1)
     spread = jnp.where(row_slot == col_slot, 1.0, 0.0).astype(jnp.bfloat16)
-    keys_t = lax.dot_general(spread, keys_ref[...], NT, preferred_element_type=jnp.float32)
+    keys_t = jnp.dot(spread, keys_ref[...], preferred_element_type=jnp.float32)
     key_inv = lax.rsqrt(jnp.sum(keys_t * keys_t, axis=1, keepdims=True) + EPS)
     key_gain = key_inv * scale_ref[0]
     keys_b = keys_t.astype(jnp.bfloat16)
@@ -153,14 +153,14 @@
     bf16 = jnp.bfloat16
     return pl.pallas_call(
         functools.partial(kernel, experts, tensors, cuts),
-        out_shape=jax.ShapeDtypeStruct(tokens.shape, bf16),
+        out_shape=pltpu.VMEM(tokens.shape, bf16),
         in_specs=[
-            pl.BlockSpec(memory_space=pl.ANY),
+            pl.BlockSpec(memory_space=pltpu.HBM),
             pl.BlockSpec(memory_space=pltpu.VMEM),
             pl.BlockSpec(memory_space=pltpu.SMEM),
-            pl.BlockSpec(memory_space=pl.ANY),
+            pl.BlockSpec(memory_space=pltpu.HBM),
             pl.BlockSpec(memory_space=pltpu.VMEM),
-            pl.BlockSpec(memory_space=pl.ANY),
+            pl.BlockSpec(memory_space=pltpu.HBM),
             pl.BlockSpec(memory_space=pltpu.VMEM),
         ],
         out_specs=pl.BlockSpec(memory_space=pltpu.VMEM),
@@ -181,8 +181,8 @@
             pltpu.SemaphoreType.DMA((len(cuts),)),
             pltpu.SemaphoreType.DMA((len(cuts),)),
         ],
-        compiler_params=pltpu.CompilerParams(collective_id=0, has_side_effects=True),
-    )(tokens, slot_keys, logit_scale.reshape(1), w_in, b_in, w_out, b_out)
+        compiler_params=pltpu.CompilerParams(collective_id=0, has_side_effects=True, vmem_limit_bytes=61 * 2**20),
+    )(tokens, slot_keys.T, logit_scale.reshape(1), w_in, b_in, w_out, b_out)
 
 
 def solution(mesh):

time: 28.3 us -> 24 us (0.85)
  local copies, waits for them, and re-layouts: 4.13 us -> 1.06 us
  Pallas kernels: 23.3 us -> 22.1 us
    unnamed x2 -> x1, local copies, waits for them, and re-layouts: 4.13 us -> 1.06 us
    pallas_call x1, Pallas kernels: 23.3 us -> 22.1 us  [local(): pl.pallas_call(functools.partial(kernel, experts, tensors, cuts), out_sha...]
where the time goes in v2:
time: 24 us; the launch traced here: 23.8 us
  Pallas kernels  22.1 us (92%)
  local copies, waits for them, and re-layouts  1.06 us (4%)
  between operations  0.66 us (3%)
    pallas_call x1, Pallas kernels, local(): pl.pallas_call(functools.partial(kernel, experts, tensors, cuts), out_sha...  22.1 us
    unnamed x1, local copies, waits for them, and re-layouts  1.06 us

profile of v2, /device:TPU:0, one launch (start us, length us, event | category | flops | bytes accessed | tf_op | source)
XLA Modules:
  0.0 23.8 jit_solution(9902503740544040411)
XLA Ops:
  0.7 22.1 %shard_map.73 = bf16[2,256,1280]{2,1,0:T(8,128)(2,1)S(1)} custom-call(bf16[2,256,1280]{2,1,0:T(8,128)(2,1)} %tokens_hbm.1, bf16[16,1280]{1,0:T(8,128)(2,1)} %bitcast.3, f32[1]{0:T(128)} %bitcast.2.scale_ref, bf16[1,1280,1792]{2,1,0:T(8,128)(2,1)} %w_in_hbm.1, bf16[1,1792]{1,0:T(2,128)(2,1)} %b_in_ref.1, bf16[1,1792,1280]{2,1,0:T(8,128)(2,1)} %w_out_hbm.1, ...), custom_call_target="tpu_custom_call" | custom-call | tf_op jit(solution)/shard_map/pallas_call | solution.py:154
  22.7 1.1 %copy.9 = bf16[2,256,1280]{2,1,0:T(8,128)(2,1)} copy(bf16[2,256,1280]{2,1,0:T(8,128)(2,1)S(1)} %shard_map.73) | data formatting | bytes 2621440

commit v3 on v2

--- a/solution.py
+++ b/solution.py
@@ -10,11 +10,6 @@
 EPS = 1e-06
 MESH = pl.DeviceIdType.MESH
 NT = (((1,), (1,)), ((), ()))
-
-
-def column_cuts(width):
-    first = (width * 3 // 5) // 256 * 256
-    return [(0, first), (first, width - first)] if 0 < first < width else [(0, width)]
 
 
 def kernel(
@@ -99,9 +94,7 @@
 
     loads[1].wait()
     pltpu.make_async_copy(recv1, recv1, recv_sem1).wait()
-    for k in range(devices):
-        x2[k * images:(k + 1) * images, :] = recv1[k]
-    x = x2[...]
+    x = recv1[...].reshape(devices * images, width)
     half = w_in.shape[1]
     for c in range(0, half, 256):
         size = min(256, half - c)
@@ -116,8 +109,7 @@
         y = jnp.dot(h, w_out[:, start:start + size], preferred_element_type=jnp.float32)
         y = y + b_out_ref[:, start:start + size].astype(jnp.float32) * first_half
         y = y.astype(jnp.bfloat16)
-        for k in range(devices):
-            send2[c][k] = y[k * images:(k + 1) * images]
+        send2[c][...] = y.reshape(devices, images, size)
         pltpu.make_async_copy(send2[c].at[me], recv2[c].at[home], recv_sem2.at[c]).start()
 
         @pl.loop(1, devices)
@@ -132,9 +124,7 @@
     cm = comb[...]
     for c, (start, size) in enumerate(cuts):
         pltpu.make_async_copy(recv2[c], recv2[c], recv_sem2.at[c]).wait()
-        for k in range(devices):
-            x2[k * images:(k + 1) * images, start:start + size] = recv2[c][k]
-        mixed = jnp.dot(cm, x2[:, start:start + size], preferred_element_type=jnp.float32)
+        mixed = jnp.dot(cm, recv2[c][...].reshape(devices * images, size), preferred_element_type=jnp.float32)
         out_ref[:, :, start:start + size] = mixed.astype(jnp.bfloat16).reshape(images, seq, size)
 
     first = recv1.at[pl.ds(0, devices - 1)]
@@ -149,7 +139,7 @@
     slots = slot_keys.shape[1]
     half = w_in.shape[2]
     devices = experts * tensors
-    cuts = column_cuts(width)
+    cuts = [(0, width)]
     bf16 = jnp.bfloat16
     return pl.pallas_call(
         functools.partial(kernel, experts, tensors, cuts),

time: 24 us -> 23.2 us (0.967)
  Pallas kernels: 22.1 us -> 21.3 us
    pallas_call x1, Pallas kernels: 22.1 us -> 21.3 us  [local(): pl.pallas_call(functools.partial(kernel, experts, tensors, cuts), out_sha...]
where the time goes in v3:
time: 23.2 us; the launch traced here: 23 us
  Pallas kernels  21.3 us (92%)
  local copies, waits for them, and re-layouts  1.06 us (5%)
  between operations  0.66 us (3%)
    pallas_call x1, Pallas kernels, local(): pl.pallas_call(functools.partial(kernel, experts, tensors, cuts), out_sha...  21.3 us
    unnamed x1, local copies, waits for them, and re-layouts  1.06 us

profile of v3, /device:TPU:0, one launch (start us, length us, event | category | flops | bytes accessed | tf_op | source)
XLA Modules:
  0.0 23.0 jit_solution(7527595345838734450)
XLA Ops:
  0.7 21.3 %shard_map.73 = bf16[2,256,1280]{2,1,0:T(8,128)(2,1)S(1)} custom-call(bf16[2,256,1280]{2,1,0:T(8,128)(2,1)} %tokens_hbm.1, bf16[16,1280]{1,0:T(8,128)(2,1)} %bitcast.3, f32[1]{0:T(128)} %bitcast.2.scale_ref, bf16[1,1280,1792]{2,1,0:T(8,128)(2,1)} %w_in_hbm.1, bf16[1,1792]{1,0:T(2,128)(2,1)} %b_in_ref.1, bf16[1,1792,1280]{2,1,0:T(8,128)(2,1)} %w_out_hbm.1, ...), custom_call_target="tpu_custom_call" | custom-call | tf_op jit(solution)/shard_map/pallas_call | solution.py:144
  22.0 1.1 %copy.9 = bf16[2,256,1280]{2,1,0:T(8,128)(2,1)} copy(bf16[2,256,1280]{2,1,0:T(8,128)(2,1)S(1)} %shard_map.73) | data formatting | bytes 2621440
